TPU v7x, 32 devices: a whole 2x2x4 slice. The times are simulated.
32 devices in a mesh: row: 4 (over z), col: 8 (over y, x, core).
Axes of the slice: x: 2, y: 2, z: 4, core: 2. Of those that a mesh axis runs over, the one named last changes fastest.
Arguments:
- right_side: float32 [16, 1024, 3072], P(None, 'row', 'col'), may hold values from -100 to 100
- cond_x: float32 [1024, 3072], P('row', 'col'), may hold values from 0.25 to 4
- cond_y: float32 [1024, 3072], P('row', 'col'), may hold values from 0.25 to 4
- pad_mask: int32 [1024, 3072], P('row', 'col'), may hold values 0 or 1
Outputs:
- solution: float32 [16, 1024, 3072], P(None, 'row', 'col')
- residual: float32 [16, 1024, 3072], P(None, 'row', 'col')
All inputs are finite; a program needn't handle non-finite values. No bound on the sum of `pad_mask` on one device may be relied on, other than what follows from the above.
Results may differ from a plain program's by a relative error of at most 0.0003.
Values sent between devices are 32-bit elements; how exact they have to be, the bound alone decides.
A program may use at most 128 MiB of HBM per device.

v0:
```python
import jax
import jax.numpy as jnp
from jax import lax
from jax.sharding import PartitionSpec as P

ITERS = 3
exact_precision = lax.Precision.HIGHEST


def passed_along(shard, axis, by):
    peers = lax.axis_size(axis)
    pairs = [(i, i + by) for i in range(peers) if 0 <= i + by < peers]
    return lax.ppermute(shard, axis, pairs)


def extended(cells, sides, width):
    for axis, dim in sides:
        count = lax.axis_size(axis)
        ends = count - 1
        head = lax.slice_in_dim(cells, 0, width, axis=dim)
        tail = lax.slice_in_dim(cells, cells.shape[dim] - width, cells.shape[dim], axis=dim)
        cells = jnp.concatenate(
            [
                lax.ppermute(tail, axis, [(i, (i + 1) % count) for i in range(ends)]),
                cells,
                lax.ppermute(head, axis, [((i + 1) % count, i) for i in range(ends)]),
            ],
            axis=dim,
        )
    return cells


def neighbour_sum(padded, cond_x, cond_above, cond_y, cond_left):
    total = cond_x * padded[:, 2:, 1:-1] + cond_above * padded[:, :-2, 1:-1]
    return total + cond_y * padded[:, 1:-1, 2:] + cond_left * padded[:, 1:-1, :-2]


def gram(left, right):
    return jnp.einsum("kab,lab->kl", left, right, precision=exact_precision)


def combine(field, matrix):
    return jnp.einsum("kab,kl->lab", field, matrix, precision=exact_precision)


def small_solve(matrix, right):
    factor = jnp.linalg.cholesky(matrix)
    return jax.scipy.linalg.cho_solve((factor, True), right)


def shards(right_side, cond_x, cond_y, pad_mask):
    pad_nodes = pad_mask.astype(jnp.float32)
    free_nodes = 1.0 - pad_nodes
    upper_row = passed_along(cond_x[-1:], "row", 1)
    cond_above = jnp.concatenate([upper_row, cond_x[:-1]], 0)
    left_column = passed_along(cond_y[:, -1:], "col", 1)
    cond_left = jnp.concatenate([left_column, cond_y[:, :-1]], 1)
    diagonal = free_nodes * (cond_x + cond_above + cond_y + cond_left) + pad_nodes
    inverse = 1.0 / diagonal
    solution = jnp.zeros_like(right_side)
    residual = right_side
    precond = residual * inverse
    direction = precond
    gram_now = lax.psum(gram(residual, precond), ("row", "col"))
    for iteration in range(ITERS):
        padded = extended(free_nodes * direction, (("row", 1), ("col", 2)), 1)
        image = pad_nodes * direction + free_nodes * (
            diagonal * direction - neighbour_sum(padded, cond_x, cond_above, cond_y, cond_left)
        )
        weighted = image * inverse
        curvature, cross_term, image_term = lax.psum(
            (gram(direction, image), gram(image, precond), gram(image, weighted)), ("row", "col")
        )
        alpha_block = small_solve(curvature, gram_now)
        solution = solution + combine(direction, alpha_block)
        residual = residual - combine(image, alpha_block)
        precond = residual * inverse
        mixed = jnp.dot(alpha_block.T, cross_term, precision=exact_precision)
        quadratic = jnp.dot(
            jnp.dot(alpha_block.T, image_term, precision=exact_precision),
            alpha_block,
            precision=exact_precision,
        )
        gram_next = gram_now - mixed - mixed.T + quadratic
        beta_block = small_solve(gram_now, gram_next)
        direction = precond + combine(direction, beta_block)
        gram_now = gram_next
    return (solution, residual)


def solution(mesh):
    in_specs = (P(None, "row", "col"), P("row", "col"), P("row", "col"), P("row", "col"))
    out_specs = (P(None, "row", "col"), P(None, "row", "col"))
    return jax.shard_map(shards, mesh=mesh, in_specs=in_specs, out_specs=out_specs, check_vma=False)
```

profile of v0, /device:TPU:0, one launch (start us, length us, event | category | flops | bytes accessed | tf_op | source)
XLA Modules:
  0.0 509.1 jit_solution(3456726133904261827)
XLA Ops:
  1.3 4.9 collective-permute-start
  9.7 2.8 multiply_add_fusion.2
  13.6 6.9 %multiply_multiply_fusion = f32[16,256,384]{2,0,1:T(8,128)S(1)} fusion(f32[16,256,384]{2,1,0:T(8,128)} %param.7, f32[256,384]{1,0:T(8,128)S(1)} %get-tuple-element.31, f32[256,384]{1,0:T(8,128)S(1)} %fusion.83), kind=kLoop, calls=%fused_computation.14 | loop fusion | flops 3145728 | bytes 13369344 | tf_op jit(solution)/shard_map/mul | solution.py:66
  20.5 3.5 collective-permute-start.3
  26.1 3.6 collective-permute-done.2
  29.7 2.7 pad_maximum_fusion.32
  32.4 2.6 copy.30
  35.0 2.6 copy.32
  37.6 3.6 collective-permute-start.5
  42.9 30.7 %fusion.78 = f32[16,16]{0,1:T(8,128)S(1)} fusion(f32[16,256,384]{2,1,0:T(8,128)} %param.7, f32[256,384]{1,0:T(8,128)S(1)} %fusion.83), kind=kOutput, calls=%fused_computation.115 | convolution fusion | flops 303562752 | bytes 6685696 | tf_op jit(solution)/shard_map/kab,lab->kl/dot_general | solution.py:39
  73.6 2.6 copy.31
  76.2 2.5 copy.33
  78.7 21.2 %fusion.14 = f32[16,256,384]{2,0,1:T(8,128)S(1)} fusion(f32[16,258,1]{2,0,1:T(8,128)} %copy.33, f32[16,1,384]{2,0,1:T(8,128)S(1)} %collective-permute-done.2, f32[16,256,384]{2,0,1:T(8,128)} %copy-done.2, f32[16,1,384]{2,0,1:T(8,128)S(1)} %collective-permute-done.3, f32[16,258,1]{2,0,1:T(8,128)} %copy.31, f32[16,256,384]{2,1,0:T(8,128)} %param.7, ...), kind=kLoop, calls=%fused_computation.17 | loop fusion | flops 33030144 | bytes 22102272 | tf_op jit(solution)/shard_map/add | solution.py:67
  99.9 8.1 %fusion.72 = f32[16,16]{1,0:T(8,128)S(1)} fusion(f32[16,256,384]{2,0,1:T(8,128)S(1)} %fusion.14, f32[256,384]{1,0:T(8,128)S(1)} %fusion.83), kind=kOutput, calls=%fused_computation.106 | convolution fusion | flops 303562752 | bytes 6685696 | tf_op jit(solution)/shard_map/kab,lab->kl/dot_general | solution.py:39
  108.1 10.6 %fusion.69 = f32[16,16]{1,0:T(8,128)S(1)} fusion(f32[16,256,384]{2,0,1:T(8,128)S(1)} %fusion.14, f32[16,256,384]{2,1,0:T(8,128)S(1)} %bitcast.144, f32[256,384]{1,0:T(8,128)S(1)} %fusion.83), kind=kOutput, calls=%fused_computation.105 | convolution fusion | flops 303562752 | bytes 12977152 | tf_op jit(solution)/shard_map/kab,lab->kl/dot_general | solution.py:39
  118.7 10.6 %fusion.66 = f32[16,16]{0,1:T(8,128)S(1)} fusion(f32[16,256,384]{2,0,1:T(8,128)S(1)} %fusion.14, f32[16,256,384]{2,1,0:T(8,128)S(1)} %bitcast.144, f32[256,384]{1,0:T(8,128)S(1)} %fusion.83), kind=kOutput, calls=%fused_computation.104 | convolution fusion | flops 303562752 | bytes 12977152 | tf_op jit(solution)/shard_map/kab,lab->kl/dot_general | solution.py:39
  129.2 45.8 %all-reduce.1 = (f32[16,16]{0,1:T(8,128)S(1)}, f32[16,16]{0,1:T(8,128)S(1)}, f32[16,16]{1,0:T(8,128)S(1)}, f32[16,16]{1,0:T(8,128)S(1)}) all-reduce(f32[16,16]{0,1:T(8,128)S(1)} %fusion.78, f32[16,16]{0,1:T(8,128)S(1)} %fusion.66, f32[16,16]{1,0:T(8,128)S(1)} %fusion.72, ...), channel_id=1, replica_groups=mesh['row'=4,'col'=8] {'row','col'}, use_global_device_ids=true, to_apply=%region_3.5 | all-reduce | flops 1024 | bytes 8192 | tf_op jit(solution)/shard_map/psum | solution.py:64
  183.6 13.2 %copy_subtract_fusion = f32[16,256,384]{2,0,1:T(8,128)} fusion(f32[16,256,384]{2,1,0:T(8,128)} %param.7, f32[16,256,384]{2,0,1:T(8,128)} %copy-done, f32[16,16]{1,0:T(8,128)S(1)} %fusion.111), kind=kOutput, calls=%fused_computation.80 | convolution fusion | flops 303562752 | bytes 18875392 | tf_op jit(solution)/shard_map/kab,kl->lab/dot_general | solution.py:43
  199.5 15.0 %broadcast_multiply_fusion.1 = (f32[16,256,384]{2,0,1:T(8,128)S(1)}, f32[16,256,384]{2,0,1:T(8,128)}) fusion(f32[256,384]{1,0:T(8,128)S(1)} %get-tuple-element.31, f32[16,16,1]{0,1,2:T(8,128)S(1)} %convolution_bitcast_fusion.4, f32[16,256,384]{2,1,0:T(8,128)} %param.7, f32[256,384]{1,0:T(8,128)S(1)} %fusion.83, f32[16,256,384]{2,0,1:T(8,128)} %copy_subtract_fusion), kind=kOutput, calls=%fused_computation.83 | convolution fusion | flops 308281344 | bytes 25953280 | tf_op jit(solution)/shard_map/kab,kl->lab/dot_general | solution.py:43
  218.9 3.7 collective-permute-done.6
  222.6 2.7 pad_maximum_fusion.29
  225.3 2.6 copy.43
  227.9 2.6 copy.45
  237.4 2.6 copy.44
  240.0 2.6 copy.46
  242.5 20.3 %fusion.31 = f32[16,256,384]{2,0,1:T(8,128)S(1)} fusion(f32[16,258,1]{2,0,1:T(8,128)} %copy.46, f32[16,1,384]{2,0,1:T(8,128)S(1)} %collective-permute-done.6, f32[16,256,384]{2,0,1:T(8,128)} %copy-done.4, f32[16,1,384]{2,0,1:T(8,128)S(1)} %collective-permute-done.7, f32[16,258,1]{2,0,1:T(8,128)} %copy.44, f32[16,256,384]{2,0,1:T(8,128)} %get-tuple-element.33, ...), kind=kLoop, calls=%fused_computation.43 | loop fusion | flops 31457280 | bytes 21709056 | tf_op jit(solution)/shard_map/add | solution.py:67
  262.9 8.1 %fusion.75 = f32[16,16]{1,0:T(8,128)S(1)} fusion(f32[16,256,384]{2,0,1:T(8,128)S(1)} %fusion.31, f32[256,384]{1,0:T(8,128)S(1)} %fusion.83), kind=kOutput, calls=%fused_computation.107 | convolution fusion | flops 303562752 | bytes 6685696 | tf_op jit(solution)/shard_map/kab,lab->kl/dot_general | solution.py:39
  271.1 8.3 %fusion.63 = f32[16,16]{1,0:T(8,128)S(1)} fusion(f32[16,256,384]{2,0,1:T(8,128)S(1)} %fusion.31, f32[16,256,384]{2,0,1:T(8,128)S(1)} %bitcast.150, f32[256,384]{1,0:T(8,128)S(1)} %fusion.83), kind=kOutput, calls=%fused_computation.103 | convolution fusion | flops 303562752 | bytes 12977152 | tf_op jit(solution)/shard_map/kab,lab->kl/dot_general | solution.py:39
  279.5 8.5 %convolution_bitcast_fusion.3 = f32[16,16]{0,1:T(8,128)S(1)} fusion(f32[16,256,384]{2,0,1:T(8,128)S(1)} %bitcast.148, f32[16,256,384]{2,0,1:T(8,128)S(1)} %fusion.31), kind=kOutput, calls=%fused_computation.112 | convolution fusion | flops 301989888 | bytes 12583936 | tf_op jit(solution)/shard_map/kab,lab->kl/dot_general | solution.py:39
  287.9 41.7 %all-reduce = (f32[16,16]{0,1:T(8,128)S(1)}, f32[16,16]{1,0:T(8,128)S(1)}, f32[16,16]{1,0:T(8,128)S(1)}) all-reduce(f32[16,16]{0,1:T(8,128)S(1)} %convolution_bitcast_fusion.3, f32[16,16]{1,0:T(8,128)S(1)} %fusion.75, f32[16,16]{1,0:T(8,128)S(1)} %fusion.63), channel_id=1, replica_groups=mesh['row'=4,'col'=8] {'row','col'}, use_global_device_ids=true, to_apply=%region_6.0 | all-reduce | flops 768 | bytes 6144 | tf_op jit(solution)/shard_map/psum | solution.py:71
  334.1 10.7 %convolution_subtract_fusion.1 = f32[16,256,384]{2,0,1:T(8,128)} fusion(f32[16,256,384]{2,0,1:T(8,128)} %copy_subtract_fusion, f32[16,256,384]{2,0,1:T(8,128)} %copy-done.1, f32[16,16]{1,0:T(8,128)S(1)} %fusion.100), kind=kOutput, calls=%fused_computation.93 | convolution fusion | flops 303562752 | bytes 18875392 | tf_op jit(solution)/shard_map/kab,kl->lab/dot_general | solution.py:43
  345.9 11.0 %broadcast_multiply_fusion = (f32[16,256,384]{2,0,1:T(8,128)S(1)}, f32[16,256,384]{2,0,1:T(8,128)}) fusion(f32[256,384]{1,0:T(8,128)S(1)} %get-tuple-element.31, f32[16,16,1]{0,1,2:T(8,128)S(1)} %convolution_bitcast_fusion.2, f32[16,256,384]{2,0,1:T(8,128)} %get-tuple-element.33, f32[16,256,384]{2,0,1:T(8,128)} %convolution_subtract_fusion.1, ...), kind=kOutput, calls=%fused_computation.82 | convolution fusion | flops 306708480 | bytes 25953280 | tf_op jit(solution)/shard_map/kab,kl->lab/dot_general | solution.py:43
  356.9 3.1 collective-permute-start.11
  361.5 4.2 collective-permute-done.10
  365.7 2.7 pad_maximum_fusion.26
  368.4 2.6 copy.54
  371.0 2.6 copy.56
  376.3 9.2 %fusion.98 = f32[16,256,384]{2,0,1:T(8,128)} fusion(f32[16,256,384]{2,0,1:T(8,128)} %get-tuple-element.33, f32[16,16]{1,0:T(8,128)S(1)} %fusion.100), kind=kOutput, calls=%fused_computation.144 | convolution fusion | flops 301989888 | bytes 12583936 | tf_op jit(solution)/shard_map/kab,kl->lab/dot_general | solution.py:43
  385.5 2.5 copy.55
  390.6 19.7 %fusion.21 = f32[16,256,384]{2,0,1:T(8,128)S(1)} fusion(f32[16,258,1]{2,0,1:T(8,128)} %copy.57, f32[16,1,384]{2,0,1:T(8,128)S(1)} %collective-permute-done.10, f32[16,256,384]{2,0,1:T(8,128)} %copy-done.3, f32[16,1,384]{2,0,1:T(8,128)S(1)} %collective-permute-done.11, f32[16,258,1]{2,0,1:T(8,128)} %copy.55, f32[16,256,384]{2,0,1:T(8,128)} %get-tuple-element.35, ...), kind=kLoop, calls=%fused_computation.25 | loop fusion | flops 31457280 | bytes 21709056 | tf_op jit(solution)/shard_map/add | solution.py:67
  410.3 2.7 copy-done.5
  413.0 10.2 %convolution_bitcast_fusion.1 = f32[16,16]{0,1:T(8,128)S(1)} fusion(f32[16,256,384]{2,0,1:T(8,128)} %get-tuple-element.35, f32[16,256,384]{2,0,1:T(8,128)S(1)} %fusion.21), kind=kOutput, calls=%fused_computation.109 | convolution fusion | flops 301989888 | bytes 12583936 | tf_op jit(solution)/shard_map/kab,lab->kl/dot_general | solution.py:39
  423.2 43.2 %psum.63 = f32[16,16]{0,1:T(8,128)S(1)} all-reduce(f32[16,16]{0,1:T(8,128)S(1)} %convolution_bitcast_fusion.1), channel_id=1, replica_groups=mesh['row'=4,'col'=8] {'row','col'}, use_global_device_ids=true, to_apply=%region_9.12 | all-reduce | flops 256 | bytes 2048 | tf_op jit(solution)/shard_map/psum | solution.py:71
  470.9 8.9 %convolution_subtract_fusion = f32[16,256,384]{2,0,1:T(8,128)S(1)} fusion(f32[16,256,384]{2,0,1:T(8,128)} %convolution_subtract_fusion.1, f32[16,16,1]{0,1,2:T(8,128)S(1)} %convolution_bitcast_fusion, f32[16,256,384]{2,0,1:T(8,128)} %copy-done.5), kind=kOutput, calls=%fused_computation.92 | convolution fusion | flops 303562752 | bytes 18875392 | tf_op jit(solution)/shard_map/kab,kl->lab/dot_general | solution.py:43
  479.9 7.6 %fusion.123 = f32[16,256,384]{2,0,1:T(8,128)S(1)} fusion(f32[16,16,1]{0,1,2:T(8,128)S(1)} %convolution_bitcast_fusion, f32[16,256,384]{2,0,1:T(8,128)} %get-tuple-element.35), kind=kOutput, calls=%fused_computation.185 | convolution fusion | flops 301989888 | bytes 12583936 | tf_op jit(solution)/shard_map/kab,kl->lab/dot_general | solution.py:43
  487.5 12.1 %add_add_fusion = f32[16,256,384]{2,0,1:T(8,128)S(1)} fusion(f32[16,256,384]{2,0,1:T(8,128)S(1)} %fusion.123, f32[16,256,384]{2,0,1:T(8,128)} %fusion.98, f32[16,256,384]{2,1,0:T(8,128)S(1)} %bitcast.146, f32[256,384]{1,0:T(8,128)S(1)} %fusion.83, f32[16,16]{1,0:T(8,128)S(1)} %fusion.111), kind=kOutput, calls=%fused_computation.72 | convolution fusion | flops 306708480 | bytes 25560064 | tf_op jit(solution)/shard_map/kab,kl->lab/dot_general | solution.py:43
  499.6 4.6 copy.62
  504.3 4.6 copy.63
  (126 shorter events, 48.3 us)
Async XLA Ops:
  1.3 8.4 %collective-permute-start = (f32[1,384]{1,0:T(1,128)S(1)}, f32[1,384]{1,0:T(1,128)S(1)}, u32[]{:S(2)}, u32[]{:S(2)}) collective-permute-start(f32[1,384]{1,0:T(1,128)S(1)} %slice.108), channel_id=1, source_target_pairs={{0,8},{8,16},{16,24},{1,9},{9,17},{17,25},{2,10},{10,18},{18,26},{... | collective-permute-start | bytes 4616 | tf_op jit(solution)/shard_map/ppermute | solution.py:13
  7.3 2.4 collective-permute-start.1
  13.6 11.7 %copy-start.12 = (s32[256,384]{1,0:T(8,128)S(1)}, s32[256,384]{1,0:T(8,128)}, u32[]{:S(2)}) copy-start(s32[256,384]{1,0:T(8,128)} %param.10) | copy-start | bytes 1179652
  20.5 9.2 %copy-start.2 = (f32[16,256,384]{2,0,1:T(8,128)}, f32[16,256,384]{2,0,1:T(8,128)S(1)}, u32[]{:S(2)}) copy-start(f32[16,256,384]{2,0,1:T(8,128)S(1)} %multiply_multiply_fusion) | copy-start | bytes 18874372
  20.5 5.6 %collective-permute-start.3 = (f32[16,1,384]{2,0,1:T(8,128)S(1)}, f32[16,1,384]{2,0,1:T(8,128)S(1)}, u32[]{:S(2)}, u32[]{:S(2)}) collective-permute-start(f32[16,1,384]{2,0,1:T(8,128)S(1)} %get-tuple-element.29), channel_id=1, source_target_pairs={{0,8},{8,16},{16,24},{1,9},{9,17},{17,25},{2,10},{10,18},{18,26},{... | collective-permute-start | bytes 73736 | tf_op jit(solution)/shard_map/ppermute | solution.py:24
  24.0 5.7 %collective-permute-start.2 = (f32[16,1,384]{2,0,1:T(8,128)S(1)}, f32[16,1,384]{2,0,1:T(8,128)S(1)}, u32[]{:S(2)}, u32[]{:S(2)}) collective-permute-start(f32[16,1,384]{2,0,1:T(8,128)S(1)} %get-tuple-element.30), channel_id=1, source_target_pairs={{8,0},{16,8},{24,16},{9,1},{17,9},{25,17},{10,2},{18,10},{26,18},{... | collective-permute-start | bytes 73736 | tf_op jit(solution)/shard_map/ppermute | solution.py:26
  37.6 41.1 %copy-start.6 = (f32[256,384]{1,0:T(8,128)S(1)}, f32[256,384]{1,0:T(8,128)}, u32[]{:S(2)}) copy-start(f32[256,384]{1,0:T(8,128)} %param.9) | copy-start | bytes 1179652
  37.6 38.6 %collective-permute-start.5 = (f32[16,258,1]{1,0,2:T(8,128)S(1)}, f32[16,258,1]{1,0,2:T(8,128)S(1)}, u32[]{:S(2)}, u32[]{:S(2)}) collective-permute-start(f32[16,258,1]{1,0,2:T(8,128)S(1)} %copy.32), channel_id=1, source_target_pairs={{0,1},{1,2},{2,3},{3,4},{4,5},{5,6},{6,7},{8,9},{9,10},{10,11},{11... | collective-permute-start | bytes 49544 | tf_op jit(solution)/shard_map/ppermute | solution.py:24
  41.3 32.4 %collective-permute-start.4 = (f32[16,258,1]{1,0,2:T(8,128)S(1)}, f32[16,258,1]{1,0,2:T(8,128)S(1)}, u32[]{:S(2)}, u32[]{:S(2)}) collective-permute-start(f32[16,258,1]{1,0,2:T(8,128)S(1)} %copy.30), channel_id=1, source_target_pairs={{1,0},{2,1},{3,2},{4,3},{5,4},{6,5},{7,6},{9,8},{10,9},{11,10},{12... | collective-permute-start | bytes 49544 | tf_op jit(solution)/shard_map/ppermute | solution.py:26
  76.2 31.8 %slice-start = ((s8[6291456]{0:T(1024)(128)(4,1)}), s8[2097152]{0:T(1024)(128)(4,1)S(1)}, s32[]{:S(2)}) async-start(s8[6291456]{0:T(1024)(128)(4,1)} %bitcast.143), calls=%async_computation | async-start | bytes 4194304
  78.7 29.3 %slice-start.1 = ((s8[6291456]{0:T(1024)(128)(4,1)}), s8[4194304]{0:T(1024)(128)(4,1)S(1)}, s32[]{:S(2)}) async-start(s8[6291456]{0:T(1024)(128)(4,1)} %bitcast.143), calls=%async_computation.1 | async-start | bytes 8388608
  99.9 18.8 %copy-start = (f32[16,256,384]{2,0,1:T(8,128)}, f32[16,256,384]{2,0,1:T(8,128)S(1)}, u32[]{:S(2)}) copy-start(f32[16,256,384]{2,0,1:T(8,128)S(1)} %fusion.14) | copy-start | bytes 18874372
  214.5 8.1 %copy-start.4 = (f32[16,256,384]{2,0,1:T(8,128)}, f32[16,256,384]{2,0,1:T(8,128)S(1)}, u32[]{:S(2)}) copy-start(f32[16,256,384]{2,0,1:T(8,128)S(1)} %get-tuple-element.32) | copy-start | bytes 18874372
  214.5 4.3 collective-permute-start.7
  216.9 5.7 %collective-permute-start.6 = (f32[16,1,384]{2,0,1:T(8,128)S(1)}, f32[16,1,384]{2,0,1:T(8,128)S(1)}, u32[]{:S(2)}, u32[]{:S(2)}) collective-permute-start(f32[16,1,384]{2,0,1:T(8,128)S(1)} %get-tuple-element.28), channel_id=1, source_target_pairs={{8,0},{16,8},{24,16},{9,1},{17,9},{25,17},{10,2},{18,10},{26,18},{... | collective-permute-start | bytes 73736 | tf_op jit(solution)/shard_map/ppermute | solution.py:26
  230.5 9.5 %collective-permute-start.9 = (f32[16,258,1]{1,0,2:T(8,128)S(1)}, f32[16,258,1]{1,0,2:T(8,128)S(1)}, u32[]{:S(2)}, u32[]{:S(2)}) collective-permute-start(f32[16,258,1]{1,0,2:T(8,128)S(1)} %copy.45), channel_id=1, source_target_pairs={{0,1},{1,2},{2,3},{3,4},{4,5},{5,6},{6,7},{8,9},{9,10},{10,11},{11... | collective-permute-start | bytes 49544 | tf_op jit(solution)/shard_map/ppermute | solution.py:24
  231.8 5.6 %collective-permute-start.8 = (f32[16,258,1]{1,0,2:T(8,128)S(1)}, f32[16,258,1]{1,0,2:T(8,128)S(1)}, u32[]{:S(2)}, u32[]{:S(2)}) collective-permute-start(f32[16,258,1]{1,0,2:T(8,128)S(1)} %copy.43), channel_id=1, source_target_pairs={{1,0},{2,1},{3,2},{4,3},{5,4},{6,5},{7,6},{9,8},{10,9},{11,10},{12... | collective-permute-start | bytes 49544 | tf_op jit(solution)/shard_map/ppermute | solution.py:26
  240.0 31.1 %slice-start.6 = ((s8[6291456]{0:T(1024)(128)(4,1)}), s8[2097152]{0:T(1024)(128)(4,1)S(1)}, s32[]{:S(2)}) async-start(s8[6291456]{0:T(1024)(128)(4,1)} %bitcast.149), calls=%async_computation.6 | async-start | bytes 4194304
  242.5 28.5 %slice-start.7 = ((s8[6291456]{0:T(1024)(128)(4,1)}), s8[4194304]{0:T(1024)(128)(4,1)S(1)}, s32[]{:S(2)}) async-start(s8[6291456]{0:T(1024)(128)(4,1)} %bitcast.149), calls=%async_computation.7 | async-start | bytes 8388608
  262.9 16.6 %copy-start.1 = (f32[16,256,384]{2,0,1:T(8,128)}, f32[16,256,384]{2,0,1:T(8,128)S(1)}, u32[]{:S(2)}) copy-start(f32[16,256,384]{2,0,1:T(8,128)S(1)} %fusion.31) | copy-start | bytes 18874372
  262.9 16.6 %slice-start.4 = ((s8[6291456]{0:T(1024)(128)(4,1)}), s8[4194304]{0:T(1024)(128)(4,1)S(1)}, s32[]{:S(2)}) async-start(s8[6291456]{0:T(1024)(128)(4,1)} %bitcast.147), calls=%async_computation.4 | async-start | bytes 8388608
  271.1 8.4 %slice-start.5 = ((s8[6291456]{0:T(1024)(128)(4,1)}), s8[2097152]{0:T(1024)(128)(4,1)S(1)}, s32[]{:S(2)}) async-start(s8[6291456]{0:T(1024)(128)(4,1)} %bitcast.147), calls=%async_computation.5 | async-start | bytes 4194304
  356.8 8.8 %copy-start.3 = (f32[16,256,384]{2,0,1:T(8,128)}, f32[16,256,384]{2,0,1:T(8,128)S(1)}, u32[]{:S(2)}) copy-start(f32[16,256,384]{2,0,1:T(8,128)S(1)} %get-tuple-element.34) | copy-start | bytes 18874372
  356.9 4.6 collective-permute-start.11
  359.9 5.7 %collective-permute-start.10 = (f32[16,1,384]{2,0,1:T(8,128)S(1)}, f32[16,1,384]{2,0,1:T(8,128)S(1)}, u32[]{:S(2)}, u32[]{:S(2)}) collective-permute-start(f32[16,1,384]{2,0,1:T(8,128)S(1)} %get-tuple-element.26), channel_id=1, source_target_pairs={{8,0},{16,8},{24,16},{9,1},{17,9},{25,17},{10,2},{18,10},{26,18},{... | collective-permute-start | bytes 73736 | tf_op jit(solution)/shard_map/ppermute | solution.py:26
  373.6 17.0 %copy-start.7 = (f32[256,384]{1,0:T(8,128)S(1)}, f32[256,384]{1,0:T(8,128)}, u32[]{:S(2)}) copy-start(f32[256,384]{1,0:T(8,128)} %param.8) | copy-start | bytes 1179652
  373.6 17.0 %copy-start.8 = (f32[256,384]{1,0:T(8,128)S(1)}, f32[256,384]{1,0:T(8,128)}, u32[]{:S(2)}) copy-start(f32[256,384]{1,0:T(8,128)} %get-tuple-element.15) | copy-start | bytes 1179652
  373.6 17.0 %copy-start.9 = (f32[256,384]{1,0:T(8,128)S(1)}, f32[256,384]{1,0:T(8,128)}, u32[]{:S(2)}) copy-start(f32[256,384]{1,0:T(8,128)} %get-tuple-element.17) | copy-start | bytes 1179652
  373.6 17.0 %copy-start.10 = (f32[256,384]{1,0:T(8,128)S(1)}, f32[256,384]{1,0:T(8,128)}, u32[]{:S(2)}) copy-start(f32[256,384]{1,0:T(8,128)} %get-tuple-element.18) | copy-start | bytes 1179652
  373.6 17.0 %copy-start.11 = (f32[256,384]{1,0:T(8,128)S(1)}, f32[256,384]{1,0:T(8,128)}, u32[]{:S(2)}) copy-start(f32[256,384]{1,0:T(8,128)} %convert_element_type.3) | copy-start | bytes 1179652
  373.6 14.4 %collective-permute-start.13 = (f32[16,258,1]{1,0,2:T(8,128)S(1)}, f32[16,258,1]{1,0,2:T(8,128)S(1)}, u32[]{:S(2)}, u32[]{:S(2)}) collective-permute-start(f32[16,258,1]{1,0,2:T(8,128)S(1)} %copy.56), channel_id=1, source_target_pairs={{0,1},{1,2},{2,3},{3,4},{4,5},{5,6},{6,7},{8,9},{9,10},{10,11},{11... | collective-permute-start | bytes 49544 | tf_op jit(solution)/shard_map/ppermute | solution.py:24
  375.0 10.5 %collective-permute-start.12 = (f32[16,258,1]{1,0,2:T(8,128)S(1)}, f32[16,258,1]{1,0,2:T(8,128)S(1)}, u32[]{:S(2)}, u32[]{:S(2)}) collective-permute-start(f32[16,258,1]{1,0,2:T(8,128)S(1)} %copy.54), channel_id=1, source_target_pairs={{1,0},{2,1},{3,2},{4,3},{5,4},{6,5},{7,6},{9,8},{10,9},{11,10},{12... | collective-permute-start | bytes 49544 | tf_op jit(solution)/shard_map/ppermute | solution.py:26
  410.3 2.7 copy-start.5
  413.0 74.5 %slice-start.2 = ((s8[6291456]{0:T(1024)(128)(4,1)}), s8[2097152]{0:T(1024)(128)(4,1)S(1)}, s32[]{:S(2)}) async-start(s8[6291456]{0:T(1024)(128)(4,1)} %bitcast.145), calls=%async_computation.2 | async-start | bytes 4194304
  470.9 16.6 %slice-start.3 = ((s8[6291456]{0:T(1024)(128)(4,1)}), s8[4194304]{0:T(1024)(128)(4,1)S(1)}, s32[]{:S(2)}) async-start(s8[6291456]{0:T(1024)(128)(4,1)} %bitcast.145), calls=%async_computation.3 | async-start | bytes 8388608
where the time goes:
time: 516 us; the launch traced here: 509 us
  matrix products  186 us (36%)
  blocking collectives  131 us (25%)
  other arithmetic  101 us (20%)
  local copies, waits for them, and re-layouts  45.3 us (9%)
  starting transfers between devices  30 us (6%)
  waiting for transfers between devices  15 us (3%)
    dot_general x8, matrix products, gram(): return jnp.einsum('kab,lab->kl', left, right, precision=exact_precision)  95.2 us
    dot_general x8, matrix products, combine(): return jnp.einsum('kab,kl->lab', field, matrix, precision=exact_precision)  87.7 us
    psum x2, blocking collectives, shards(): lax.psum((gram(direction, image), gram(image, precond), gram(image, weigh...  84.9 us
    add x3, other arithmetic, shards(): pad_nodes * direction  61.2 us
    psum x1, blocking collectives, shards(): gram_now = lax.psum(gram(residual, precond), ('row', 'col'))  45.8 us
    ppermute x6, starting transfers between devices, extended(): lax.ppermute(tail, axis, [(i, (i + 1) % count) for i in range(ends)])  15.2 us
    ppermute x6, waiting for transfers between devices, extended(): lax.ppermute(head, axis, [((i + 1) % count, i) for i in range(ends)])  14 us
    unnamed x44, local copies, waits for them, and re-layouts  12.1 us
  transfers between devices with their start and end apart: 14, of which 5 were waited for; matrix products, arithmetic and copies ran while one was open for 10% of the time, Pallas kernels for 0%

commit v1 on v0

--- a/solution.py
+++ b/solution.py
@@ -69,7 +69,8 @@
         )
         weighted = image * inverse
         curvature, cross_term, image_term = lax.psum(
-            (gram(direction, image), gram(image, precond), gram(image, weighted)), ("row", "col")
+            lax.psum((gram(direction, image), gram(image, precond), gram(image, weighted)), "col"),
+            "row",
         )
         alpha_block = small_solve(curvature, gram_now)
         solution = solution + combine(direction, alpha_block)

time: 516 us -> 518 us (level)
  blocking collectives: 131 us -> 156 us
  matrix products: 186 us -> 165 us
  starting transfers between devices: 30 us -> 23.6 us
    psum x0 -> x3, blocking collectives: none -> 45.3 us  [shards(): lax.psum(lax.psum((gram(direction, image), gram(image, precond), gram(ima...]
    dot_general x8, matrix products: 95.2 us -> 74.5 us  [gram(): return jnp.einsum('kab,lab->kl', left, right, precision=exact_precision)]
    psum x2 -> x3, blocking collectives: 84.9 us -> 67.5 us  [shards(): lax.psum((gram(direction, image), gram(image, precond), gram(image, weigh...]
    ppermute x6, starting transfers between devices: 15.2 us -> 8.74 us  [extended(): lax.ppermute(tail, axis, [(i, (i + 1) % count) for i in range(ends)])]
  transfers between devices with their start and end apart: 14 -> 14, of which waited for: 5 -> 5; matrix products, arithmetic and copies ran while one was open for 10% -> 5% of each run, Pallas kernels for 0% -> 0%
where the time goes in v1:
time: 518 us; the launch traced here: 508 us
  matrix products  165 us (32%)
  blocking collectives  156 us (30%)
  other arithmetic  101 us (19%)
  local copies, waits for them, and re-layouts  45.4 us (9%)
  starting transfers between devices  23.6 us (5%)
  waiting for transfers between devices  15 us (3%)
    dot_general x8, matrix products, combine(): return jnp.einsum('kab,kl->lab', field, matrix, precision=exact_precision)  87.7 us
    dot_general x8, matrix products, gram(): return jnp.einsum('kab,lab->kl', left, right, precision=exact_precision)  74.5 us
    psum x3, blocking collectives, shards(): lax.psum((gram(direction, image), gram(image, precond), gram(image, weigh...  67.5 us
    add x3, other arithmetic, shards(): pad_nodes * direction  60.6 us
    psum x3, blocking collectives, shards(): lax.psum(lax.psum((gram(direction, image), gram(image, precond), gram(ima...  45.3 us
    psum x1, blocking collectives, shards(): gram_now = lax.psum(gram(residual, precond), ('row', 'col'))  43.7 us
    ppermute x6, waiting for transfers between devices, extended(): lax.ppermute(head, axis, [((i + 1) % count, i) for i in range(ends)])  14.9 us
    unnamed x44, local copies, waits for them, and re-layouts  12.1 us
  transfers between devices with their start and end apart: 14, of which 5 were waited for; matrix products, arithmetic and copies ran while one was open for 5% of the time, Pallas kernels for 0%

profile of v1, /device:TPU:0, one launch (start us, length us, event | category | flops | bytes accessed | tf_op | source)
XLA Modules:
  0.0 508.5 jit_solution(15997526571833877776)
XLA Ops:
  1.5 5.2 %collective-permute-start = (f32[1,384]{1,0:T(1,128)S(1)}, f32[1,384]{1,0:T(1,128)S(1)}, u32[]{:S(2)}, u32[]{:S(2)}) collective-permute-start(f32[1,384]{1,0:T(1,128)S(1)} %slice.108), channel_id=1, source_target_pairs={{0,8},{8,16},{16,24},{1,9},{9,17},{17,25},{2,10},{10,18},{18,26},{... | collective-permute-start | bytes 4616 | tf_op jit(solution)/shard_map/ppermute | solution.py:13
  11.0 2.8 multiply_add_fusion.2
  14.8 10.1 %fusion.78 = f32[16,16]{0,1:T(8,128)S(1)} fusion(f32[16,256,384]{2,1,0:T(8,128)S(1)} %copy-done, f32[256,384]{1,0:T(8,128)S(1)} %fusion.83), kind=kOutput, calls=%fused_computation.115 | convolution fusion | flops 303562752 | bytes 6685696 | tf_op jit(solution)/shard_map/kab,lab->kl/dot_general | solution.py:39
  25.0 43.7 %psum.107 = f32[16,16]{0,1:T(8,128)S(1)} all-reduce(f32[16,16]{0,1:T(8,128)S(1)} %fusion.78), channel_id=1, replica_groups=mesh['row'=4,'col'=8] {'row','col'}, use_global_device_ids=true, to_apply=%region_4.6 | all-reduce | flops 256 | bytes 2048 | tf_op jit(solution)/shard_map/psum | solution.py:64
  70.2 6.8 %multiply_multiply_fusion = f32[16,256,384]{2,0,1:T(8,128)S(1)} fusion(f32[16,256,384]{2,1,0:T(8,128)} %param.7, f32[256,384]{1,0:T(8,128)S(1)} %get-tuple-element.36, f32[256,384]{1,0:T(8,128)S(1)} %fusion.83), kind=kLoop, calls=%fused_computation.14 | loop fusion | flops 3145728 | bytes 13369344 | tf_op jit(solution)/shard_map/mul | solution.py:66
  81.2 3.7 collective-permute-done.2
  85.0 2.7 pad_maximum_fusion.32
  87.6 2.7 copy.30
  90.3 2.6 copy.32
  99.8 2.6 copy.31
  102.4 2.5 copy.33
  104.9 21.5 %fusion.14 = f32[16,256,384]{2,0,1:T(8,128)S(1)} fusion(f32[16,258,1]{2,0,1:T(8,128)} %copy.33, f32[16,1,384]{2,0,1:T(8,128)S(1)} %collective-permute-done.2, f32[16,256,384]{2,0,1:T(8,128)} %copy-done.3, f32[16,1,384]{2,0,1:T(8,128)S(1)} %collective-permute-done.3, f32[16,258,1]{2,0,1:T(8,128)} %copy.31, f32[16,256,384]{2,1,0:T(8,128)} %param.7, ...), kind=kLoop, calls=%fused_computation.17 | loop fusion | flops 33030144 | bytes 22102272 | tf_op jit(solution)/shard_map/add | solution.py:67
  126.5 8.1 %fusion.72 = f32[16,16]{1,0:T(8,128)S(1)} fusion(f32[16,256,384]{2,0,1:T(8,128)S(1)} %fusion.14, f32[256,384]{1,0:T(8,128)S(1)} %fusion.83), kind=kOutput, calls=%fused_computation.106 | convolution fusion | flops 303562752 | bytes 6685696 | tf_op jit(solution)/shard_map/kab,lab->kl/dot_general | solution.py:39
  134.6 10.4 %fusion.69 = f32[16,16]{1,0:T(8,128)S(1)} fusion(f32[16,256,384]{2,0,1:T(8,128)S(1)} %fusion.14, f32[16,256,384]{2,1,0:T(8,128)S(1)} %bitcast.144, f32[256,384]{1,0:T(8,128)S(1)} %fusion.83), kind=kOutput, calls=%fused_computation.105 | convolution fusion | flops 303562752 | bytes 12977152 | tf_op jit(solution)/shard_map/kab,lab->kl/dot_general | solution.py:39
  145.0 10.6 %fusion.66 = f32[16,16]{0,1:T(8,128)S(1)} fusion(f32[16,256,384]{2,0,1:T(8,128)S(1)} %fusion.14, f32[16,256,384]{2,1,0:T(8,128)S(1)} %bitcast.144, f32[256,384]{1,0:T(8,128)S(1)} %fusion.83), kind=kOutput, calls=%fused_computation.104 | convolution fusion | flops 303562752 | bytes 12977152 | tf_op jit(solution)/shard_map/kab,lab->kl/dot_general | solution.py:39
  155.6 25.3 %all-reduce.1 = (f32[16,16]{0,1:T(8,128)S(1)}, f32[16,16]{1,0:T(8,128)S(1)}, f32[16,16]{1,0:T(8,128)S(1)}) all-reduce(f32[16,16]{0,1:T(8,128)S(1)} %fusion.66, f32[16,16]{1,0:T(8,128)S(1)} %fusion.72, f32[16,16]{1,0:T(8,128)S(1)} %fusion.69), channel_id=1, replica_groups=mesh['row'=4,'col'=8] {'col'}, use_global_device_ids=true, to_apply=%region_0.0 | all-reduce | flops 768 | bytes 6144 | tf_op jit(solution)/shard_map/psum | solution.py:72
  180.9 17.3 %all-reduce.3 = (f32[16,16]{0,1:T(8,128)S(1)}, f32[16,16]{1,0:T(8,128)S(1)}, f32[16,16]{1,0:T(8,128)S(1)}) all-reduce(f32[16,16]{0,1:T(8,128)S(1)} %get-tuple-element.11, f32[16,16]{1,0:T(8,128)S(1)} %get-tuple-element.12, f32[16,16]{1,0:T(8,128)S(1)} %get-tuple-element.13), channel_id=1, replica_groups=mesh['row'=4,'col'=8] {'row'}, use_global_device_ids=true, to_apply=%region_1.0 | all-reduce | flops 768 | bytes 6144 | tf_op jit(solution)/shard_map/psum | solution.py:71
  202.6 13.2 %copy_subtract_fusion = f32[16,256,384]{2,0,1:T(8,128)} fusion(f32[16,256,384]{2,1,0:T(8,128)} %param.7, f32[16,256,384]{2,0,1:T(8,128)} %copy-done.2, f32[16,16]{1,0:T(8,128)S(1)} %fusion.111), kind=kOutput, calls=%fused_computation.80 | convolution fusion | flops 303562752 | bytes 18875392 | tf_op jit(solution)/shard_map/kab,kl->lab/dot_general | solution.py:43
  218.5 15.0 %broadcast_multiply_fusion.1 = (f32[16,256,384]{2,0,1:T(8,128)S(1)}, f32[16,256,384]{2,0,1:T(8,128)}) fusion(f32[256,384]{1,0:T(8,128)S(1)} %get-tuple-element.36, f32[16,16,1]{0,1,2:T(8,128)S(1)} %convolution_bitcast_fusion.4, f32[16,256,384]{2,1,0:T(8,128)} %param.7, f32[256,384]{1,0:T(8,128)S(1)} %fusion.83, f32[16,256,384]{2,0,1:T(8,128)} %copy_subtract_fusion), kind=kOutput, calls=%fused_computation.83 | convolution fusion | flops 308281344 | bytes 25953280 | tf_op jit(solution)/shard_map/kab,kl->lab/dot_general | solution.py:43
  236.8 3.7 collective-permute-done.6
  240.6 2.7 pad_maximum_fusion.29
  243.2 2.6 copy.43
  245.8 2.6 copy.45
  254.1 2.6 copy.44
  256.7 2.6 copy.46
  259.2 19.8 %fusion.31 = f32[16,256,384]{2,0,1:T(8,128)S(1)} fusion(f32[16,258,1]{2,0,1:T(8,128)} %copy.46, f32[16,1,384]{2,0,1:T(8,128)S(1)} %collective-permute-done.6, f32[16,256,384]{2,0,1:T(8,128)} %copy-done.5, f32[16,1,384]{2,0,1:T(8,128)S(1)} %collective-permute-done.7, f32[16,258,1]{2,0,1:T(8,128)} %copy.44, f32[16,256,384]{2,0,1:T(8,128)} %get-tuple-element.38, ...), kind=kLoop, calls=%fused_computation.43 | loop fusion | flops 31457280 | bytes 21709056 | tf_op jit(solution)/shard_map/add | solution.py:67
  279.0 8.1 %fusion.75 = f32[16,16]{1,0:T(8,128)S(1)} fusion(f32[16,256,384]{2,0,1:T(8,128)S(1)} %fusion.31, f32[256,384]{1,0:T(8,128)S(1)} %fusion.83), kind=kOutput, calls=%fused_computation.107 | convolution fusion | flops 303562752 | bytes 6685696 | tf_op jit(solution)/shard_map/kab,lab->kl/dot_general | solution.py:39
  287.2 8.3 %fusion.63 = f32[16,16]{1,0:T(8,128)S(1)} fusion(f32[16,256,384]{2,0,1:T(8,128)S(1)} %fusion.31, f32[16,256,384]{2,0,1:T(8,128)S(1)} %bitcast.150, f32[256,384]{1,0:T(8,128)S(1)} %fusion.83), kind=kOutput, calls=%fused_computation.103 | convolution fusion | flops 303562752 | bytes 12977152 | tf_op jit(solution)/shard_map/kab,lab->kl/dot_general | solution.py:39
  295.6 8.6 %convolution_bitcast_fusion.3 = f32[16,16]{0,1:T(8,128)S(1)} fusion(f32[16,256,384]{2,0,1:T(8,128)S(1)} %bitcast.148, f32[16,256,384]{2,0,1:T(8,128)S(1)} %fusion.31), kind=kOutput, calls=%fused_computation.112 | convolution fusion | flops 301989888 | bytes 12583936 | tf_op jit(solution)/shard_map/kab,lab->kl/dot_general | solution.py:39
  304.2 26.3 %all-reduce = (f32[16,16]{0,1:T(8,128)S(1)}, f32[16,16]{1,0:T(8,128)S(1)}, f32[16,16]{1,0:T(8,128)S(1)}) all-reduce(f32[16,16]{0,1:T(8,128)S(1)} %convolution_bitcast_fusion.3, f32[16,16]{1,0:T(8,128)S(1)} %fusion.75, f32[16,16]{1,0:T(8,128)S(1)} %fusion.63), channel_id=1, replica_groups=mesh['row'=4,'col'=8] {'col'}, use_global_device_ids=true, to_apply=%region_9.0 | all-reduce | flops 768 | bytes 6144 | tf_op jit(solution)/shard_map/psum | solution.py:72
  330.4 17.5 %all-reduce.2 = (f32[16,16]{0,1:T(8,128)S(1)}, f32[16,16]{1,0:T(8,128)S(1)}, f32[16,16]{1,0:T(8,128)S(1)}) all-reduce(f32[16,16]{0,1:T(8,128)S(1)} %get-tuple-element.8, f32[16,16]{1,0:T(8,128)S(1)} %get-tuple-element.9, f32[16,16]{1,0:T(8,128)S(1)} %get-tuple-element.10), channel_id=1, replica_groups=mesh['row'=4,'col'=8] {'row'}, use_global_device_ids=true, to_apply=%region_10.0 | all-reduce | flops 768 | bytes 6144 | tf_op jit(solution)/shard_map/psum | solution.py:71
  352.4 10.7 %convolution_subtract_fusion.1 = f32[16,256,384]{2,0,1:T(8,128)} fusion(f32[16,256,384]{2,0,1:T(8,128)} %copy_subtract_fusion, f32[16,256,384]{2,0,1:T(8,128)} %copy-done.1, f32[16,16]{1,0:T(8,128)S(1)} %fusion.100), kind=kOutput, calls=%fused_computation.93 | convolution fusion | flops 303562752 | bytes 18875392 | tf_op jit(solution)/shard_map/kab,kl->lab/dot_general | solution.py:43
  364.2 11.0 %broadcast_multiply_fusion = (f32[16,256,384]{2,0,1:T(8,128)S(1)}, f32[16,256,384]{2,0,1:T(8,128)}) fusion(f32[256,384]{1,0:T(8,128)S(1)} %get-tuple-element.36, f32[16,16,1]{0,1,2:T(8,128)S(1)} %convolution_bitcast_fusion.2, f32[16,256,384]{2,0,1:T(8,128)} %get-tuple-element.38, f32[16,256,384]{2,0,1:T(8,128)} %convolution_subtract_fusion.1, ...), kind=kOutput, calls=%fused_computation.82 | convolution fusion | flops 306708480 | bytes 25953280 | tf_op jit(solution)/shard_map/kab,kl->lab/dot_general | solution.py:43
  378.2 4.0 collective-permute-done.10
  382.2 2.7 pad_maximum_fusion.26
  384.8 2.6 copy.54
  387.4 2.6 copy.56
  392.8 9.1 %fusion.98 = f32[16,256,384]{2,0,1:T(8,128)} fusion(f32[16,256,384]{2,0,1:T(8,128)} %get-tuple-element.38, f32[16,16]{1,0:T(8,128)S(1)} %fusion.100), kind=kOutput, calls=%fused_computation.144 | convolution fusion | flops 301989888 | bytes 12583936 | tf_op jit(solution)/shard_map/kab,kl->lab/dot_general | solution.py:43
  407.0 19.3 %fusion.21 = f32[16,256,384]{2,0,1:T(8,128)S(1)} fusion(f32[16,258,1]{2,0,1:T(8,128)} %copy.57, f32[16,1,384]{2,0,1:T(8,128)S(1)} %collective-permute-done.10, f32[16,256,384]{2,0,1:T(8,128)} %copy-done.4, f32[16,1,384]{2,0,1:T(8,128)S(1)} %collective-permute-done.11, f32[16,258,1]{2,0,1:T(8,128)} %copy.55, f32[16,256,384]{2,0,1:T(8,128)} %get-tuple-element.40, ...), kind=kLoop, calls=%fused_computation.25 | loop fusion | flops 31457280 | bytes 21709056 | tf_op jit(solution)/shard_map/add | solution.py:67
  426.4 2.7 copy-done.6
  429.1 10.2 %convolution_bitcast_fusion.1 = f32[16,16]{0,1:T(8,128)S(1)} fusion(f32[16,256,384]{2,0,1:T(8,128)} %get-tuple-element.40, f32[16,256,384]{2,0,1:T(8,128)S(1)} %fusion.21), kind=kOutput, calls=%fused_computation.109 | convolution fusion | flops 301989888 | bytes 12583936 | tf_op jit(solution)/shard_map/kab,lab->kl/dot_general | solution.py:39
  439.3 15.9 %psum.118 = f32[16,16]{0,1:T(8,128)S(1)} all-reduce(f32[16,16]{0,1:T(8,128)S(1)} %convolution_bitcast_fusion.1), channel_id=1, replica_groups=mesh['row'=4,'col'=8] {'col'}, use_global_device_ids=true, to_apply=%region_15.18 | all-reduce | flops 256 | bytes 2048 | tf_op jit(solution)/shard_map/psum | solution.py:72
  455.2 10.5 %psum.119 = f32[16,16]{0,1:T(8,128)S(1)} all-reduce(f32[16,16]{0,1:T(8,128)S(1)} %psum.118), channel_id=1, replica_groups=mesh['row'=4,'col'=8] {'row'}, use_global_device_ids=true, to_apply=%region_16.19 | all-reduce | flops 256 | bytes 2048 | tf_op jit(solution)/shard_map/psum | solution.py:71
  470.3 8.9 %convolution_subtract_fusion = f32[16,256,384]{2,0,1:T(8,128)S(1)} fusion(f32[16,256,384]{2,0,1:T(8,128)} %convolution_subtract_fusion.1, f32[16,16,1]{0,1,2:T(8,128)S(1)} %convolution_bitcast_fusion, f32[16,256,384]{2,0,1:T(8,128)} %copy-done.6), kind=kOutput, calls=%fused_computation.92 | convolution fusion | flops 303562752 | bytes 18875392 | tf_op jit(solution)/shard_map/kab,kl->lab/dot_general | solution.py:43
  479.2 7.6 %fusion.123 = f32[16,256,384]{2,0,1:T(8,128)S(1)} fusion(f32[16,16,1]{0,1,2:T(8,128)S(1)} %convolution_bitcast_fusion, f32[16,256,384]{2,0,1:T(8,128)} %get-tuple-element.40), kind=kOutput, calls=%fused_computation.185 | convolution fusion | flops 301989888 | bytes 12583936 | tf_op jit(solution)/shard_map/kab,kl->lab/dot_general | solution.py:43
  486.9 12.1 %add_add_fusion = f32[16,256,384]{2,0,1:T(8,128)S(1)} fusion(f32[16,256,384]{2,0,1:T(8,128)S(1)} %fusion.123, f32[16,256,384]{2,0,1:T(8,128)} %fusion.98, f32[16,256,384]{2,1,0:T(8,128)S(1)} %bitcast.146, f32[256,384]{1,0:T(8,128)S(1)} %fusion.83, f32[16,16]{1,0:T(8,128)S(1)} %fusion.111), kind=kOutput, calls=%fused_computation.72 | convolution fusion | flops 306708480 | bytes 25560064 | tf_op jit(solution)/shard_map/kab,kl->lab/dot_general | solution.py:43
  499.0 4.6 copy.62
  503.6 4.6 copy.63
  (131 shorter events, 55.7 us)
Async XLA Ops:
  0.6 14.2 %copy-start = (f32[16,256,384]{2,1,0:T(8,128)S(1)}, f32[16,256,384]{2,1,0:T(8,128)}, u32[]{:S(2)}) copy-start(f32[16,256,384]{2,1,0:T(8,128)} %param.7) | copy-start | bytes 18874372
  1.5 9.5 %collective-permute-start = (f32[1,384]{1,0:T(1,128)S(1)}, f32[1,384]{1,0:T(1,128)S(1)}, u32[]{:S(2)}, u32[]{:S(2)}) collective-permute-start(f32[1,384]{1,0:T(1,128)S(1)} %slice.108), channel_id=1, source_target_pairs={{0,8},{8,16},{16,24},{1,9},{9,17},{17,25},{2,10},{10,18},{18,26},{... | collective-permute-start | bytes 4616 | tf_op jit(solution)/shard_map/ppermute | solution.py:13
  7.7 3.3 collective-permute-start.1
  77.1 7.9 %copy-start.3 = (f32[16,256,384]{2,0,1:T(8,128)}, f32[16,256,384]{2,0,1:T(8,128)S(1)}, u32[]{:S(2)}) copy-start(f32[16,256,384]{2,0,1:T(8,128)S(1)} %multiply_multiply_fusion) | copy-start | bytes 18874372
  77.1 4.2 collective-permute-start.3
  79.2 5.7 %collective-permute-start.2 = (f32[16,1,384]{2,0,1:T(8,128)S(1)}, f32[16,1,384]{2,0,1:T(8,128)S(1)}, u32[]{:S(2)}, u32[]{:S(2)}) collective-permute-start(f32[16,1,384]{2,0,1:T(8,128)S(1)} %get-tuple-element.35), channel_id=1, source_target_pairs={{8,0},{16,8},{24,16},{9,1},{17,9},{25,17},{10,2},{18,10},{26,18},{... | collective-permute-start | bytes 73736 | tf_op jit(solution)/shard_map/ppermute | solution.py:26
  87.6 17.3 %copy-start.7 = (f32[256,384]{1,0:T(8,128)S(1)}, f32[256,384]{1,0:T(8,128)}, u32[]{:S(2)}) copy-start(f32[256,384]{1,0:T(8,128)} %param.9) | copy-start | bytes 1179652
  92.9 9.5 %collective-permute-start.5 = (f32[16,258,1]{1,0,2:T(8,128)S(1)}, f32[16,258,1]{1,0,2:T(8,128)S(1)}, u32[]{:S(2)}, u32[]{:S(2)}) collective-permute-start(f32[16,258,1]{1,0,2:T(8,128)S(1)} %copy.32), channel_id=1, source_target_pairs={{0,1},{1,2},{2,3},{3,4},{4,5},{5,6},{6,7},{8,9},{9,10},{10,11},{11... | collective-permute-start | bytes 49544 | tf_op jit(solution)/shard_map/ppermute | solution.py:24
  94.2 5.6 %collective-permute-start.4 = (f32[16,258,1]{1,0,2:T(8,128)S(1)}, f32[16,258,1]{1,0,2:T(8,128)S(1)}, u32[]{:S(2)}, u32[]{:S(2)}) collective-permute-start(f32[16,258,1]{1,0,2:T(8,128)S(1)} %copy.30), channel_id=1, source_target_pairs={{1,0},{2,1},{3,2},{4,3},{5,4},{6,5},{7,6},{9,8},{10,9},{11,10},{12... | collective-permute-start | bytes 49544 | tf_op jit(solution)/shard_map/ppermute | solution.py:26
  102.4 32.2 %slice-start = ((s8[6291456]{0:T(1024)(128)(4,1)}), s8[2097152]{0:T(1024)(128)(4,1)S(1)}, s32[]{:S(2)}) async-start(s8[6291456]{0:T(1024)(128)(4,1)} %bitcast.143), calls=%async_computation | async-start | bytes 4194304
  104.9 29.7 %slice-start.1 = ((s8[6291456]{0:T(1024)(128)(4,1)}), s8[4194304]{0:T(1024)(128)(4,1)S(1)}, s32[]{:S(2)}) async-start(s8[6291456]{0:T(1024)(128)(4,1)} %bitcast.143), calls=%async_computation.1 | async-start | bytes 8388608
  126.5 18.5 %copy-start.2 = (f32[16,256,384]{2,0,1:T(8,128)}, f32[16,256,384]{2,0,1:T(8,128)S(1)}, u32[]{:S(2)}) copy-start(f32[16,256,384]{2,0,1:T(8,128)S(1)} %fusion.14) | copy-start | bytes 18874372
  233.5 7.0 %copy-start.5 = (f32[16,256,384]{2,0,1:T(8,128)}, f32[16,256,384]{2,0,1:T(8,128)S(1)}, u32[]{:S(2)}) copy-start(f32[16,256,384]{2,0,1:T(8,128)S(1)} %get-tuple-element.37) | copy-start | bytes 18874372
  233.5 3.3 collective-permute-start.7
  234.8 5.7 %collective-permute-start.6 = (f32[16,1,384]{2,0,1:T(8,128)S(1)}, f32[16,1,384]{2,0,1:T(8,128)S(1)}, u32[]{:S(2)}, u32[]{:S(2)}) collective-permute-start(f32[16,1,384]{2,0,1:T(8,128)S(1)} %get-tuple-element.33), channel_id=1, source_target_pairs={{8,0},{16,8},{24,16},{9,1},{17,9},{25,17},{10,2},{18,10},{26,18},{... | collective-permute-start | bytes 73736 | tf_op jit(solution)/shard_map/ppermute | solution.py:26
  248.4 8.2 %collective-permute-start.9 = (f32[16,258,1]{1,0,2:T(8,128)S(1)}, f32[16,258,1]{1,0,2:T(8,128)S(1)}, u32[]{:S(2)}, u32[]{:S(2)}) collective-permute-start(f32[16,258,1]{1,0,2:T(8,128)S(1)} %copy.45), channel_id=1, source_target_pairs={{0,1},{1,2},{2,3},{3,4},{4,5},{5,6},{6,7},{8,9},{9,10},{10,11},{11... | collective-permute-start | bytes 49544 | tf_op jit(solution)/shard_map/ppermute | solution.py:24
  249.7 4.4 collective-permute-start.8
  256.7 30.5 %slice-start.6 = ((s8[6291456]{0:T(1024)(128)(4,1)}), s8[2097152]{0:T(1024)(128)(4,1)S(1)}, s32[]{:S(2)}) async-start(s8[6291456]{0:T(1024)(128)(4,1)} %bitcast.149), calls=%async_computation.6 | async-start | bytes 4194304
  259.2 27.9 %slice-start.7 = ((s8[6291456]{0:T(1024)(128)(4,1)}), s8[4194304]{0:T(1024)(128)(4,1)S(1)}, s32[]{:S(2)}) async-start(s8[6291456]{0:T(1024)(128)(4,1)} %bitcast.149), calls=%async_computation.7 | async-start | bytes 8388608
  279.0 16.5 %copy-start.1 = (f32[16,256,384]{2,0,1:T(8,128)}, f32[16,256,384]{2,0,1:T(8,128)S(1)}, u32[]{:S(2)}) copy-start(f32[16,256,384]{2,0,1:T(8,128)S(1)} %fusion.31) | copy-start | bytes 18874372
  279.0 16.6 %slice-start.4 = ((s8[6291456]{0:T(1024)(128)(4,1)}), s8[4194304]{0:T(1024)(128)(4,1)S(1)}, s32[]{:S(2)}) async-start(s8[6291456]{0:T(1024)(128)(4,1)} %bitcast.147), calls=%async_computation.4 | async-start | bytes 8388608
  287.2 8.4 %slice-start.5 = ((s8[6291456]{0:T(1024)(128)(4,1)}), s8[2097152]{0:T(1024)(128)(4,1)S(1)}, s32[]{:S(2)}) async-start(s8[6291456]{0:T(1024)(128)(4,1)} %bitcast.147), calls=%async_computation.5 | async-start | bytes 4194304
  375.1 7.0 %copy-start.4 = (f32[16,256,384]{2,0,1:T(8,128)}, f32[16,256,384]{2,0,1:T(8,128)S(1)}, u32[]{:S(2)}) copy-start(f32[16,256,384]{2,0,1:T(8,128)S(1)} %get-tuple-element.39) | copy-start | bytes 18874372
  375.1 3.0 collective-permute-start.11
  376.4 5.7 %collective-permute-start.10 = (f32[16,1,384]{2,0,1:T(8,128)S(1)}, f32[16,1,384]{2,0,1:T(8,128)S(1)}, u32[]{:S(2)}, u32[]{:S(2)}) collective-permute-start(f32[16,1,384]{2,0,1:T(8,128)S(1)} %get-tuple-element.31), channel_id=1, source_target_pairs={{8,0},{16,8},{24,16},{9,1},{17,9},{25,17},{10,2},{18,10},{26,18},{... | collective-permute-start | bytes 73736 | tf_op jit(solution)/shard_map/ppermute | solution.py:26
  390.0 17.0 %copy-start.8 = (f32[256,384]{1,0:T(8,128)S(1)}, f32[256,384]{1,0:T(8,128)}, u32[]{:S(2)}) copy-start(f32[256,384]{1,0:T(8,128)} %param.8) | copy-start | bytes 1179652
  390.0 17.0 %copy-start.9 = (f32[256,384]{1,0:T(8,128)S(1)}, f32[256,384]{1,0:T(8,128)}, u32[]{:S(2)}) copy-start(f32[256,384]{1,0:T(8,128)} %convert_element_type.3) | copy-start | bytes 1179652
  390.1 17.0 %copy-start.10 = (f32[256,384]{1,0:T(8,128)S(1)}, f32[256,384]{1,0:T(8,128)}, u32[]{:S(2)}) copy-start(f32[256,384]{1,0:T(8,128)} %get-tuple-element.20) | copy-start | bytes 1179652
  390.1 17.0 %copy-start.11 = (f32[256,384]{1,0:T(8,128)S(1)}, f32[256,384]{1,0:T(8,128)}, u32[]{:S(2)}) copy-start(f32[256,384]{1,0:T(8,128)} %get-tuple-element.22) | copy-start | bytes 1179652
  390.1 17.0 %copy-start.12 = (f32[256,384]{1,0:T(8,128)S(1)}, f32[256,384]{1,0:T(8,128)}, u32[]{:S(2)}) copy-start(f32[256,384]{1,0:T(8,128)} %get-tuple-element.23) | copy-start | bytes 1179652
  390.1 14.4 %collective-permute-start.13 = (f32[16,258,1]{1,0,2:T(8,128)S(1)}, f32[16,258,1]{1,0,2:T(8,128)S(1)}, u32[]{:S(2)}, u32[]{:S(2)}) collective-permute-start(f32[16,258,1]{1,0,2:T(8,128)S(1)} %copy.56), channel_id=1, source_target_pairs={{0,1},{1,2},{2,3},{3,4},{4,5},{5,6},{6,7},{8,9},{9,10},{10,11},{11... | collective-permute-start | bytes 49544 | tf_op jit(solution)/shard_map/ppermute | solution.py:24
  391.5 10.4 %collective-permute-start.12 = (f32[16,258,1]{1,0,2:T(8,128)S(1)}, f32[16,258,1]{1,0,2:T(8,128)S(1)}, u32[]{:S(2)}, u32[]{:S(2)}) collective-permute-start(f32[16,258,1]{1,0,2:T(8,128)S(1)} %copy.54), channel_id=1, source_target_pairs={{1,0},{2,1},{3,2},{4,3},{5,4},{6,5},{7,6},{9,8},{10,9},{11,10},{12... | collective-permute-start | bytes 49544 | tf_op jit(solution)/shard_map/ppermute | solution.py:26
  426.4 2.7 copy-start.6
  429.1 57.8 %slice-start.2 = ((s8[6291456]{0:T(1024)(128)(4,1)}), s8[2097152]{0:T(1024)(128)(4,1)S(1)}, s32[]{:S(2)}) async-start(s8[6291456]{0:T(1024)(128)(4,1)} %bitcast.145), calls=%async_computation.2 | async-start | bytes 4194304
  470.3 16.6 %slice-start.3 = ((s8[6291456]{0:T(1024)(128)(4,1)}), s8[4194304]{0:T(1024)(128)(4,1)S(1)}, s32[]{:S(2)}) async-start(s8[6291456]{0:T(1024)(128)(4,1)} %bitcast.145), calls=%async_computation.3 | async-start | bytes 8388608
